TPU v7x, 32 devices: a whole 2x2x4 slice. The times are simulated.
32 devices in a mesh: ep: 8 (over z, x), corner: 4 (over y, core).
Axes of the slice: x: 2, y: 2, z: 4, core: 2. Of those that a mesh axis runs over, the one named last changes fastest.
Arguments:
- required: float32 [8, 262144], P('corner', 'ep'), may hold values from -3 to 3
- arrival: float32 [8, 262144], P('corner', 'ep'), may hold values from -7.2 to 7.2
- hold_required: float32 [8, 262144], P('corner', 'ep'), may hold values from -5.4 to 5.4
- early_arrival: float32 [8, 262144], P('corner', 'ep'), may hold values from -3 to 3
- part_ids: int32 [262144], P('ep'), may hold values from 0 to 63
- bin_edges: int32 [512], replicated, may hold values from -4096 to -1, as said below
Outputs:
- part_hist: float32 [64, 8, 2, 512], P(None, 'corner')
- part_tns: float32 [64, 8, 2], P(None, 'corner')
- part_share: float32 [64], replicated
- tns: float32 [8, 2], P('corner')
- wns: float32 [8, 2], P('corner')
- worst: float32 [2, 262144], P(None, 'ep')
Inputs may be any that keep to these rules, and one draw needn't show every extreme that they name: `bin_edges`: strictly increasing and negative; consecutive nodes differ by 1 to 8.
All inputs are finite; a program needn't handle non-finite values.
Results may differ from a plain program's by a relative error of at most 0.0003.
Values sent between devices are 32-bit elements; how exact they have to be, the bound alone decides.
A program may use at most 64 MiB of HBM per device.

v0:
```python
import jax
import jax.numpy as jnp
from jax import lax
from jax.sharding import PartitionSpec as P

GROUPS = 64


def node_tables(bin_edges):
    nodes = bin_edges.astype(jnp.float32) * 0.001
    upper = jnp.concatenate([nodes[1:], jnp.zeros((1,), jnp.float32)])
    lower = jnp.concatenate([nodes[:1] - 1.0, nodes[:-1]])
    return (nodes, lower, upper)


def on_device(required, arrival, hold_required, early_arrival, part_ids, bin_edges):
    corner_count, rows = required.shape
    endpoints = rows * lax.axis_size("ep")
    nodes, lower, upper = node_tables(bin_edges)
    setup = required - arrival
    hold = early_arrival - hold_required
    worst_pair = lax.pmin((jnp.min(setup, axis=0), jnp.min(hold, axis=0)), "corner")
    worst = jnp.stack(worst_pair, axis=0)
    both = jnp.stack([setup, hold], axis=1)
    block = min(4096, rows)
    labels = jnp.arange(GROUPS, dtype=jnp.int32)
    node_col = nodes[None, :, None]
    low_col = lower[None, :, None]
    high_col = upper[None, :, None]
    rise_den = node_col - low_col
    fall_den = high_col - node_col
    contract = (((1,), (1,)), ((), ()))

    def one_block(index, carry):
        hist, stats, counts = carry
        start = index * block
        ids_block = lax.dynamic_slice_in_dim(part_ids, start, block, 0)
        member = labels[:, None] == ids_block[None, :]
        member_low = member.astype(jnp.bfloat16)
        member_full = member.astype(jnp.float32)
        slab = lax.dynamic_slice_in_dim(both, start, block, 2)
        level = jnp.clip(slab, nodes[0], 0.0).reshape(corner_count * 2, 1, block)
        weight = jnp.maximum(
            jnp.minimum((level - low_col) / rise_den, (high_col - level) / fall_den), 0.0
        )
        weight = weight.astype(jnp.bfloat16)
        product = jnp.einsum("pe,kbe->pkb", member_low, weight, preferred_element_type=jnp.float32)
        hist = hist + product.reshape(GROUPS, corner_count, 2, nodes.shape[0])
        negative = jnp.minimum(slab, 0.0).reshape(corner_count * 2, block)
        part_neg = lax.dot_general(
            member_full,
            negative,
            contract,
            precision=lax.Precision.HIGHEST,
            preferred_element_type=jnp.float32,
        )
        stats = stats + part_neg.reshape(GROUPS, corner_count, 2)
        counts = counts + jnp.sum(member_full, axis=1)
        return (hist, stats, counts)

    start_state = (
        jnp.zeros((GROUPS, corner_count, 2, nodes.shape[0]), jnp.float32),
        jnp.zeros((GROUPS, corner_count, 2), jnp.float32),
        jnp.zeros((GROUPS,), jnp.float32),
    )
    hist, stats, counts = lax.fori_loop(0, rows // block, one_block, start_state)
    local_min = jnp.stack([jnp.min(setup, axis=1), jnp.min(hold, axis=1)], axis=1)
    wns = lax.pmin(local_min, "ep")
    hist, stats, counts = lax.psum((hist, stats, counts), "ep")
    tns_raw = jnp.sum(stats, axis=0)
    density = GROUPS * nodes.shape[0] / endpoints
    share = GROUPS / endpoints
    part_hist = hist * density
    part_tns = stats * share
    part_share = counts * share
    tns = tns_raw * (1.0 / endpoints)
    return (part_hist, part_tns, part_share, tns, wns, worst)


def solution(mesh):
    in_specs = (
        P("corner", "ep"),
        P("corner", "ep"),
        P("corner", "ep"),
        P("corner", "ep"),
        P("ep"),
        P(),
    )
    out_specs = (
        P(None, "corner", None, None),
        P(None, "corner", None),
        P(),
        P("corner", None),
        P("corner", None),
        P(None, "ep"),
    )
    return jax.shard_map(
        on_device, mesh=mesh, in_specs=in_specs, out_specs=out_specs, check_vma=False
    )
```

profile of v0, /device:TPU:0, one launch (start us, length us, event | category | flops | bytes accessed | tf_op | source)
XLA Modules:
  0.0 186.4 jit_solution(7004410176938454817)
XLA Ops:
  7.2 2.9 %fusion.19 = (f32[32768]{0:T(1024)}, f32[2]{0:T(128)}, f32[2,32768]{1,0:T(2,128)S(1)}, f32[2]{0:T(128)}, f32[32768]{0:T(1024)}, /*index=5*/f32[2,32768]{1,0:T(2,128)S(1)}) fusion(f32[2,32768]{1,0:T(2,128)} %param.8, f32[2,32768]{1,0:T(2,128)} %param.9, f32[2,32768]{1,0:T(2,128)} %param.11, f32[2,32768]{1,0:T(2,128)} %param.10), kind=kLoop, calls=%fused_computation.32 | loop fusion | flops 327676 | bytes 1835024 | tf_op jit(solution)/shard_map/reduce_min | solution.py:22
  10.2 0.5 slice.16
  12.4 88.2 %while.18 = (s32[]{:T(128)}, f32[64,2,2,512]{3,0,2,1:T(8,128)S(1)}, f32[64,2,2]{0,2,1:T(2,128)S(1)}, f32[64]{0:T(128)S(1)}, s32[32768]{0:T(1024)}, /*index=5*/f3...) while((s32[]{:T(128)}, f32[64,2,2,512]{3,0,2,1:T(8,128)S(1)}, ...), condition=%wide.region_2.0_spmd.clone, body=%wide.region_0.2_spmd.clone.sunk | while | flops 1146667648 | bytes 2584807 | solution.py:66
  12.4 0.5 slice.23
  12.9 0.7 dynamic_slice.26
  13.8 0.6 convolution_add_fusion.2
  14.5 0.7 maximum_minimum_fusion.2
  15.2 8.0 %fusion.32 = f32[64,4,512]{2,0,1:T(8,128)S(1)} fusion(f32[512]{0:T(512)S(1)} %bitcast.40, f32[512]{0:T(512)S(1)} %bitcast.42, f32[512]{0:T(512)S(1)} %bitcast.44, f32[512]{0:T(512)S(1)} %bitcast.46, f32[4,4096]{1,0:T(4,128)S(1)} %sub.129, s32[4096]{0:T(1024)S(1)} %dynamic_slice.26), kind=kOutput, calls=%fused_computation.2.clone.1 | convolution fusion | flops 1132724224 | bytes 614400 | tf_op jit(solution)/shard_map/while/body/eval_jaxpr/pe,kbe->pkb/dot_general | solution.py:47
  23.4 0.5 slice.23
  23.9 0.7 dynamic_slice.26
  24.9 0.6 convolution_add_fusion.2
  25.5 0.7 maximum_minimum_fusion.2
  26.3 8.0 %fusion.32 = f32[64,4,512]{2,0,1:T(8,128)S(1)} fusion(f32[512]{0:T(512)S(1)} %bitcast.40, f32[512]{0:T(512)S(1)} %bitcast.42, f32[512]{0:T(512)S(1)} %bitcast.44, f32[512]{0:T(512)S(1)} %bitcast.46, f32[4,4096]{1,0:T(4,128)S(1)} %sub.129, s32[4096]{0:T(1024)S(1)} %dynamic_slice.26), kind=kOutput, calls=%fused_computation.2.clone.1 | convolution fusion | flops 1132724224 | bytes 614400 | tf_op jit(solution)/shard_map/while/body/eval_jaxpr/pe,kbe->pkb/dot_general | solution.py:47
  34.4 0.5 slice.23
  34.9 0.7 dynamic_slice.26
  35.9 0.6 convolution_add_fusion.2
  36.5 0.7 maximum_minimum_fusion.2
  37.3 8.0 %fusion.32 = f32[64,4,512]{2,0,1:T(8,128)S(1)} fusion(f32[512]{0:T(512)S(1)} %bitcast.40, f32[512]{0:T(512)S(1)} %bitcast.42, f32[512]{0:T(512)S(1)} %bitcast.44, f32[512]{0:T(512)S(1)} %bitcast.46, f32[4,4096]{1,0:T(4,128)S(1)} %sub.129, s32[4096]{0:T(1024)S(1)} %dynamic_slice.26), kind=kOutput, calls=%fused_computation.2.clone.1 | convolution fusion | flops 1132724224 | bytes 614400 | tf_op jit(solution)/shard_map/while/body/eval_jaxpr/pe,kbe->pkb/dot_general | solution.py:47
  46.0 0.7 dynamic_slice.26
  46.9 0.6 convolution_add_fusion.2
  47.6 0.7 maximum_minimum_fusion.2
  48.3 8.0 %fusion.32 = f32[64,4,512]{2,0,1:T(8,128)S(1)} fusion(f32[512]{0:T(512)S(1)} %bitcast.40, f32[512]{0:T(512)S(1)} %bitcast.42, f32[512]{0:T(512)S(1)} %bitcast.44, f32[512]{0:T(512)S(1)} %bitcast.46, f32[4,4096]{1,0:T(4,128)S(1)} %sub.129, s32[4096]{0:T(1024)S(1)} %dynamic_slice.26), kind=kOutput, calls=%fused_computation.2.clone.1 | convolution fusion | flops 1132724224 | bytes 614400 | tf_op jit(solution)/shard_map/while/body/eval_jaxpr/pe,kbe->pkb/dot_general | solution.py:47
  57.0 0.7 dynamic_slice.26
  57.9 0.6 convolution_add_fusion.2
  58.6 0.7 maximum_minimum_fusion.2
  59.3 8.0 %fusion.32 = f32[64,4,512]{2,0,1:T(8,128)S(1)} fusion(f32[512]{0:T(512)S(1)} %bitcast.40, f32[512]{0:T(512)S(1)} %bitcast.42, f32[512]{0:T(512)S(1)} %bitcast.44, f32[512]{0:T(512)S(1)} %bitcast.46, f32[4,4096]{1,0:T(4,128)S(1)} %sub.129, s32[4096]{0:T(1024)S(1)} %dynamic_slice.26), kind=kOutput, calls=%fused_computation.2.clone.1 | convolution fusion | flops 1132724224 | bytes 614400 | tf_op jit(solution)/shard_map/while/body/eval_jaxpr/pe,kbe->pkb/dot_general | solution.py:47
  68.0 0.7 dynamic_slice.26
  69.0 0.6 convolution_add_fusion.2
  69.6 0.7 maximum_minimum_fusion.2
  70.4 8.0 %fusion.32 = f32[64,4,512]{2,0,1:T(8,128)S(1)} fusion(f32[512]{0:T(512)S(1)} %bitcast.40, f32[512]{0:T(512)S(1)} %bitcast.42, f32[512]{0:T(512)S(1)} %bitcast.44, f32[512]{0:T(512)S(1)} %bitcast.46, f32[4,4096]{1,0:T(4,128)S(1)} %sub.129, s32[4096]{0:T(1024)S(1)} %dynamic_slice.26), kind=kOutput, calls=%fused_computation.2.clone.1 | convolution fusion | flops 1132724224 | bytes 614400 | tf_op jit(solution)/shard_map/while/body/eval_jaxpr/pe,kbe->pkb/dot_general | solution.py:47
  79.0 0.7 dynamic_slice.26
  80.0 0.6 convolution_add_fusion.2
  80.6 0.7 maximum_minimum_fusion.2
  81.4 8.0 %fusion.32 = f32[64,4,512]{2,0,1:T(8,128)S(1)} fusion(f32[512]{0:T(512)S(1)} %bitcast.40, f32[512]{0:T(512)S(1)} %bitcast.42, f32[512]{0:T(512)S(1)} %bitcast.44, f32[512]{0:T(512)S(1)} %bitcast.46, f32[4,4096]{1,0:T(4,128)S(1)} %sub.129, s32[4096]{0:T(1024)S(1)} %dynamic_slice.26), kind=kOutput, calls=%fused_computation.2.clone.1 | convolution fusion | flops 1132724224 | bytes 614400 | tf_op jit(solution)/shard_map/while/body/eval_jaxpr/pe,kbe->pkb/dot_general | solution.py:47
  90.1 0.7 dynamic_slice.26
  91.0 0.6 convolution_add_fusion.2
  91.6 0.7 maximum_minimum_fusion.2
  92.4 8.0 %fusion.32 = f32[64,4,512]{2,0,1:T(8,128)S(1)} fusion(f32[512]{0:T(512)S(1)} %bitcast.40, f32[512]{0:T(512)S(1)} %bitcast.42, f32[512]{0:T(512)S(1)} %bitcast.44, f32[512]{0:T(512)S(1)} %bitcast.46, f32[4,4096]{1,0:T(4,128)S(1)} %sub.129, s32[4096]{0:T(1024)S(1)} %dynamic_slice.26), kind=kOutput, calls=%fused_computation.2.clone.1 | convolution fusion | flops 1132724224 | bytes 614400 | tf_op jit(solution)/shard_map/while/body/eval_jaxpr/pe,kbe->pkb/dot_general | solution.py:47
  100.6 1.2 copy.12
  101.8 23.5 %pmin.21 = f32[2,2]{0,1:T(2,128)S(1)} all-reduce(f32[2,2]{0,1:T(2,128)S(1)} %pad_maximum_fusion.4), channel_id=1, replica_groups=mesh['ep'=8,'corner'=4] {'ep'}, use_global_device_ids=true, to_apply=%region_9.10 | all-reduce | flops 4 | bytes 32 | tf_op jit(solution)/shard_map/pmin | solution.py:68
  125.3 0.7 copy.13
  126.0 17.2 %all-reduce = (f32[64,2,2]{0,2,1:T(2,128)S(1)}, f32[64]{0:T(128)S(1)}) all-reduce(f32[64,2,2]{0,2,1:T(2,128)S(1)} %get-tuple-element.208, f32[64]{0:T(128)S(1)} %get-tuple-element.209), channel_id=1, replica_groups=mesh['ep'=8,'corner'=4] {'ep'}, use_global_device_ids=true, to_apply=%region_4.5 | all-reduce | flops 320 | bytes 2560 | tf_op jit(solution)/shard_map/psum | solution.py:69
  143.2 0.5 broadcast_multiply_fusion.3
  143.7 0.6 fusion.21
  144.3 0.6 broadcast_multiply_fusion.2
  144.9 1.9 %pad_maximum_fusion.1 = f32[2,32768]{1,0:T(2,128)} fusion(f32[1,32768]{1,0:T(1,128)} %get-tuple-element.282, f32[1,32768]{1,0:T(1,128)} %get-tuple-element.283), kind=kLoop, calls=%fused_computation.21 | loop fusion | flops 65536 | bytes 524288 | tf_op jit(solution)/shard_map/stack | solution.py:23
  146.8 30.8 %all-reduce.5.cloned.1.call-done = f32[64,2,2,512]{3,2,1,0:T(2,128)} async-done(((f32[64,2,2,512]{3,2,1,0:T(2,128)}), f32[64,2,2,512]{3,2,1,0:T(2,128)}) %all-reduce.5.cloned.1.call-update) | async-done | bytes 524304 | tf_op jit(solution)/shard_map/psum | solution.py:69
  177.5 2.1 %broadcast_multiply_fusion = f32[64,2,2,512]{3,2,1,0:T(2,128)} fusion(f32[64,2,2,512]{3,2,1,0:T(2,128)} %all-reduce.5.cloned.1.call-done), kind=kLoop, calls=%fused_computation.22 | loop fusion | flops 131072 | bytes 1048576 | tf_op jit(solution)/shard_map/mul | solution.py:73
  (58 shorter events, 7.4 us)
Async XLA Ops:
  7.2 3.0 %copy-start = (s32[512]{0:T(512)S(1)}, s32[512]{0:T(512)}, u32[]{:S(2)}) copy-start(s32[512]{0:T(512)} %param.13) | copy-start | bytes 6148
  7.2 137.7 %all-reduce.7.cloned.1.call-start = ((), (), s32[]{:S(2)}) async-start(), calls=%async_computation.1 | async-start | bytes 524288 | tf_op jit(solution)/shard_map/pmin | solution.py:22
  10.1 167.4 %all-reduce.5.cloned.1.call-start = ((), (), s32[]{:S(2)}) async-start(), calls=%async_computation | async-start | bytes 1048576 | tf_op jit(solution)/shard_map/psum | solution.py:69
  100.6 1.2 copy-start.1
  100.6 1.2 copy-start.2
Sparse Core Ops, SparseCore 0:
  11.0 35.2 all-reduce.6
  101.9 75.5 all-reduce.4
where the time goes:
time: 187 us; the launch traced here: 186 us
  matrix products  68.7 us (37%)
  blocking collectives  40.7 us (22%)
  waiting for transfers between devices  30.8 us (16%)
  other arithmetic  17.8 us (10%)
  between operations  14.8 us (8%)
  local copies, waits for them, and re-layouts  13.1 us (7%)
    dot_general x8, matrix products, one_block(): jnp.einsum('pe,kbe->pkb', member_low, weight, preferred_element_type=jnp....  63.7 us
    psum x1, waiting for transfers between devices, on_device(): hist, stats, counts = lax.psum((hist, stats, counts), 'ep')  30.8 us
    pmin x1, blocking collectives, on_device(): wns = lax.pmin(local_min, 'ep')  23.5 us
    psum x1, blocking collectives, on_device(): hist, stats, counts = lax.psum((hist, stats, counts), 'ep')  17.2 us
    dynamic_slice x8, local copies, waits for them, and re-layouts, one_block(): ids_block = lax.dynamic_slice_in_dim(part_ids, start, block, 0)  5.75 us
    min x8, other arithmetic, one_block(): level = jnp.clip(slab, nodes[0], 0.0).reshape(corner_count * 2, 1, block)  5.49 us
    dot_general x8, matrix products, one_block(): lax.dot_general(member_full, negative, contract, precision=lax.Precision....  5.07 us
    slice x8, local copies, waits for them, and re-layouts, one_block(): level = jnp.clip(slab, nodes[0], 0.0).reshape(corner_count * 2, 1, block)  4.11 us
  transfers between devices with their start and end apart: 2, of which 1 were waited for; matrix products, arithmetic and copies ran while one was open for 51% of the time, Pallas kernels for 0%

commit v1 on v0

v1 whole, which is shorter than its diff:
```python
import functools
import jax
import jax.numpy as jnp
from jax import lax
from jax.experimental import pallas as pl
from jax.experimental.pallas import tpu as pltpu
from jax.sharding import PartitionSpec as P

GROUPS = 64
HIGH = 4
LANES = 128
EXTRA = 16
HALF = 512
MESH = pl.DeviceIdType.MESH


def pick(table, index):
    return jnp.take_along_axis(table, index, axis=1, mode="promise_in_bounds")


def make_tables(edges_ref):
    nodes = edges_ref[...].astype(jnp.float32) * 0.001
    lane = lax.broadcasted_iota(jnp.int32, (8, LANES), 1)
    rows = [jnp.broadcast_to(nodes[q : q + 1], (8, LANES)) for q in range(4)]
    third = []
    for j in range(8):
        index = (8 * lane + j) & 127
        parts = [pick(row, index) for row in rows]
        value = parts[3]
        for q in (2, 1, 0):
            value = jnp.where(lane < 16 * (q + 1), parts[q], value)
        third.append(value)
    following = pick(third[0], jnp.minimum(lane + 1, LANES - 1))
    third.append(jnp.where(lane >= 63, 0.0, following))
    second = [pick(third[0], (8 * lane + j) & 63) for j in range(1, 8)]
    first = [pick(third[0], jnp.full((8, LANES), 8 * i, jnp.int32)) for i in range(1, 8)]
    lowest = pick(third[0], jnp.zeros((8, LANES), jnp.int32))
    return first, second, third, lowest


def search(tables, slack):
    first, second, third, lowest = tables
    level = jnp.minimum(jnp.maximum(slack, lowest), 0.0)
    group = jnp.zeros(level.shape, jnp.int32)
    for bound in first:
        group += (level >= bound).astype(jnp.int32)
    finer = group * 8
    for table in second:
        finer += (level >= pick(table, group)).astype(jnp.int32)
    index = finer * 8
    low = pick(third[0], finer)
    high = pick(third[8], finer)
    inner = [pick(table, finer) for table in third[1:8]]
    for value in inner:
        above = level >= value
        index += above.astype(jnp.int32)
        low = jnp.where(above, value, low)
    for value in reversed(inner):
        high = jnp.where(level < value, value, high)
    scale = 1.0 / (high - low)
    return index, (high - level) * scale, (level - low) * scale


def compute_kernel(req, arr, hreq, early, ids, edges, hist_out, stats_out, worst_out, acc, least):
    corners, rows = req.shape
    combos = 2 * corners
    halves = 8 // combos
    depth = halves * HALF
    tables = make_tables(edges)
    acc[...] = jnp.zeros_like(acc)
    least[...] = jnp.full_like(least, jnp.inf)
    narrow = jnp.bfloat16
    iota = lax.broadcasted_iota(jnp.int32, (16, depth), 0)
    iota_low = iota.astype(jnp.float32).astype(narrow)
    zero = jnp.zeros((16, depth), narrow)
    one = jnp.ones((16, depth), narrow)

    def block(step, carry):
        slabs, parts = [], []
        for half in range(halves):
            at = pl.ds(pl.multiple_of(step * depth + half * HALF, HALF), HALF)
            setup = req[:, at] - arr[:, at]
            hold = early[:, at] - hreq[:, at]
            worst_out[0:1, at] = jnp.min(setup, axis=0, keepdims=True)
            worst_out[1:2, at] = jnp.min(hold, axis=0, keepdims=True)
            slabs += [setup, hold]
            parts.append(jnp.broadcast_to(ids[:, at], (combos, HALF)))
        slab = jnp.concatenate(slabs, axis=0)
        part = jnp.concatenate(parts, axis=0)
        low_at, code, w_first, w_second = [], [], [], []
        smallest = least[...]
        for lane in range(0, HALF, LANES):
            piece = slab[:, lane : lane + LANES]
            smallest = jnp.minimum(smallest, piece)
            index, wa, wb = search(tables, piece)
            low_at.append((index & (LANES - 1)).astype(jnp.float32))
            code.append(((index >> 7) * GROUPS + part[:, lane : lane + LANES]).astype(jnp.float32))
            w_first.append(wa)
            w_second.append(wb)
        least[...] = smallest
        low_at, code, w_first, w_second = (
            jnp.concatenate(v, axis=1) for v in (low_at, code, w_first, w_second)
        )
        neg = jnp.minimum(slab, 0.0)
        piece_a = neg.astype(narrow).astype(jnp.float32)
        rest = neg - piece_a
        piece_b = rest.astype(narrow).astype(jnp.float32)
        piece_c = rest - piece_b
        for r in range(combos):

            def spread(v):
                row = jnp.concatenate(
                    [v[r + combos * h : r + combos * h + 1] for h in range(halves)], axis=1
                )
                return jnp.broadcast_to(row, (16, depth)).astype(narrow)

            at_low, at_code, wa, wb = (spread(v) for v in (low_at, code, w_first, w_second))
            left = []
            for start in range(0, LANES, 16):
                row = iota_low + narrow(start)
                next_row = iota_low + narrow(start - 1)
                left.append(
                    jnp.where(at_low == row, wa, jnp.where(at_low == next_row, wb, zero))
                )
            tail = jnp.where(at_low == narrow(LANES - 1), wb, zero)
            tail = jnp.where(iota_low == narrow(0), tail, zero)
            for place, v in ((1, piece_a), (2, piece_b), (3, piece_c)):
                tail = jnp.where(iota_low == narrow(place), spread(v), tail)
            tail = jnp.where(iota_low == narrow(4), one, tail)
            left.append(tail)
            left = jnp.concatenate(left, axis=0)
            right = jnp.concatenate(
                [
                    jnp.where(at_code == iota_low + narrow(start), one, zero)
                    for start in range(0, HIGH * GROUPS, 16)
                ],
                axis=0,
            )
            acc[r] += lax.dot_general(
                left, right, (((1,), (1,)), ((), ())), preferred_element_type=jnp.float32
            )
        return carry

    lax.fori_loop(0, rows // depth, block, 0)

    lane = lax.broadcasted_iota(jnp.int32, (1, HIGH * GROUPS), 1)
    stats_out[...] = jnp.zeros_like(stats_out)

    def fold(v):
        v = v[:, :LANES] + v[:, LANES:]
        return v + pltpu.roll(jnp.broadcast_to(v, (8, LANES)), GROUPS, 1)[0:1]

    for r in range(combos):
        over = jnp.broadcast_to(acc[r, LANES : LANES + 1], (8, HIGH * GROUPS))
        over = pltpu.roll(over, GROUPS, 1)[0:1]
        acc[r, 0:1] += jnp.where(lane >= GROUPS, over, 0.0)
        turned = acc[r, 0:LANES].T
        for g in range(HIGH):
            hist_out[r * GROUPS : (r + 1) * GROUPS, g * LANES : (g + 1) * LANES] = turned[
                g * GROUPS : (g + 1) * GROUPS
            ]
        total = (
            acc[r, LANES + 1 : LANES + 2]
            + acc[r, LANES + 2 : LANES + 3]
            + acc[r, LANES + 3 : LANES + 4]
        )
        stats_out[r : r + 1] = fold(total)
    stats_out[combos : combos + 1] = fold(acc[0, LANES + 4 : LANES + 5])
    stats_out[8:16] = jnp.broadcast_to(jnp.min(least[...], axis=1, keepdims=True), (8, LANES))


def exchange_kernel(
    n, nc, density,
    hist, stats, worst, hist_out, stats_out, worst_out,
    hist_in, stats_in, worst_in,
    hs, hr, gs, gr, ss, sr, ws, wr, vs, vr,
):
    me = lax.axis_index("ep")
    mc = lax.axis_index("corner")
    chunk = hist.shape[0] // n
    width = worst.shape[1] // nc
    barrier = pltpu.get_barrier_semaphore()
    for d in range(1, n):
        pl.semaphore_signal(
            barrier, inc=1, device_id={"ep": lax.rem(me + d, n)}, device_id_type=MESH
        )
    for d in range(1, nc):
        pl.semaphore_signal(
            barrier, inc=1, device_id={"corner": lax.rem(mc + d, nc)}, device_id_type=MESH
        )
    pl.semaphore_wait(barrier, n - 1 + nc - 1)

    def send(src, dst, s_sem, r_sem, target):
        copy = pltpu.make_async_remote_copy(
            src_ref=src, dst_ref=dst, send_sem=s_sem, recv_sem=r_sem,
            device_id=target, device_id_type=MESH,
        )
        copy.start()
        return copy

    def lanes(k):
        return pl.ds(pl.multiple_of(k * width, LANES), width)

    def rows(k):
        return pl.ds(pl.multiple_of(k * chunk, 8), chunk)

    scatter, shares, mins = [], [], []
    for d in range(1, nc):
        t = lax.rem(mc + d, nc)
        mins.append(
            send(worst.at[:, lanes(t)], worst_in.at[d], ws.at[d], wr.at[d], {"corner": t})
        )
    for d in range(1, n):
        t = lax.rem(me + d, n)
        scatter.append(send(hist.at[rows(t)], hist_in.at[d], hs.at[d], hr.at[d], {"ep": t}))
    for d in range(1, n):
        t = lax.rem(me + d, n)
        shares.append(send(stats, stats_in.at[me], ss.at[d], sr.at[d], {"ep": t}))

    for copy in mins:
        copy.wait_recv()
    low = worst[:, lanes(mc)]
    for d in range(1, nc):
        low = jnp.minimum(low, worst_in[d])
    worst_out[:, lanes(mc)] = low
    spread = []
    for d in range(1, nc):
        t = lax.rem(mc + d, nc)
        part = worst_out.at[:, lanes(mc)]
        spread.append(send(part, part, vs.at[d], vr.at[d], {"corner": t}))

    total = hist[rows(me)]
    for d in range(1, n):
        scatter[d - 1].wait_recv()
        total += hist_in[d]
    hist_out[rows(me)] = total * density
    gather = []
    for d in range(1, n):
        t = lax.rem(me + d, n)
        part = hist_out.at[rows(me)]
        gather.append(send(part, part, gs.at[d], gr.at[d], {"ep": t}))

    for copy in shares:
        copy.wait_recv()
    stats_in[me] = stats[...]
    added = stats_in[0, 0:8]
    least = stats_in[0, 8:16]
    for k in range(1, n):
        added += stats_in[k, 0:8]
        least = jnp.minimum(least, stats_in[k, 8:16])
    stats_out[0:8] = added
    stats_out[8:16] = least
    for copy in spread + gather:
        copy.wait_recv()
    for copy in mins + scatter + shares + spread + gather:
        copy.wait_send()


def on_device(required, arrival, hold_required, early_arrival, part_ids, bin_edges):
    corners, rows = required.shape
    n, nc = lax.axis_size("ep"), lax.axis_size("corner")
    endpoints = rows * n
    bins = bin_edges.shape[0]
    combos = 2 * corners
    f32 = jnp.float32
    vmem = pl.BlockSpec(memory_space=pltpu.VMEM)
    shapes = (
        jax.ShapeDtypeStruct((combos * GROUPS, bins), f32),
        jax.ShapeDtypeStruct((16, LANES), f32),
        jax.ShapeDtypeStruct((2, rows), f32),
    )
    hist, stats, worst = pl.pallas_call(
        compute_kernel,
        out_shape=shapes,
        in_specs=[vmem] * 6,
        out_specs=[vmem] * 3,
        scratch_shapes=[
            pltpu.VMEM((combos, LANES + EXTRA, HIGH * GROUPS), f32),
            pltpu.VMEM((8, LANES), f32),
        ],
        name="local_report",
    )(
        required, arrival, hold_required, early_arrival,
        part_ids.reshape(1, rows), bin_edges.reshape(bins // LANES, LANES),
    )
    dma = pltpu.SemaphoreType.DMA
    hist, stats, worst = pl.pallas_call(
        functools.partial(exchange_kernel, n, nc, GROUPS * bins / endpoints),
        out_shape=shapes,
        in_specs=[vmem] * 3,
        out_specs=[vmem] * 3,
        scratch_shapes=[
            pltpu.VMEM((n, combos * GROUPS // n, bins), f32),
            pltpu.VMEM((n, 16, LANES), f32),
            pltpu.VMEM((nc, 2, rows // nc), f32),
        ]
        + [dma((n,))] * 6
        + [dma((nc,))] * 4,
        compiler_params=pltpu.CompilerParams(collective_id=0, has_side_effects=True),
        name="exchange",
    )(hist, stats, worst)
    part_hist = hist.reshape(2, corners, GROUPS, bins).transpose(2, 1, 0, 3)
    share = GROUPS / endpoints
    sums = stats[:combos, :GROUPS].reshape(2, corners, GROUPS)
    part_tns = sums.transpose(2, 1, 0) * share
    part_share = stats[combos, :GROUPS] * share
    tns = jnp.sum(sums, axis=2).T * (1.0 / endpoints)
    least = jnp.min(stats[8:16, 0].reshape(8 // combos, 2, corners), axis=0)
    return (part_hist, part_tns, part_share, tns, least.T, worst)


def solution(mesh):
    in_specs = (
        P("corner", "ep"),
        P("corner", "ep"),
        P("corner", "ep"),
        P("corner", "ep"),
        P("ep"),
        P(),
    )
    out_specs = (
        P(None, "corner", None, None),
        P(None, "corner", None),
        P(),
        P("corner", None),
        P("corner", None),
        P(None, "ep"),
    )
    return jax.shard_map(
        on_device, mesh=mesh, in_specs=in_specs, out_specs=out_specs, check_vma=False
    )
```

time: 187 us -> 77.8 us (0.42)
  the two profiles are of different devices: /device:TPU:0 before, /device:TPU:31 now
where the time goes in v1:
time: 77.8 us; the launch traced here: 77.6 us
  Pallas kernels  71.1 us (91%)
  local copies, waits for them, and re-layouts  5.15 us (7%)
    pallas_call x1, Pallas kernels, on_device(): pl.pallas_call(compute_kernel, out_shape=shapes, in_specs=[vmem] * 6, out...  38.9 us
    pallas_call x1, Pallas kernels, on_device(): pl.pallas_call(functools.partial(exchange_kernel, n, nc, GROUPS * bins /...  32.2 us
    reshape x1, local copies, waits for them, and re-layouts, on_device(): part_hist = hist.reshape(2, corners, GROUPS, bins).transpose(2, 1, 0, 3)  2.28 us
    unnamed x7, local copies, waits for them, and re-layouts  2.01 us

profile of v1, /device:TPU:31, one launch (start us, length us, event | category | flops | bytes accessed | tf_op | source)
XLA Modules:
  0.0 77.6 jit_solution(2379490026995805422)
XLA Ops:
  0.6 38.9 %local_report.1 = (f32[256,512]{1,0:T(8,128)}, f32[16,128]{1,0:T(8,128)}, f32[2,32768]{1,0:T(2,128)}) custom-call(f32[2,32768]{1,0:T(2,128)} %req.1, f32[2,32768]{1,0:T(2,128)} %arr.1, f32[2,32768]{1,0:T(2,128)} %hreq.1, f32[2,32768]{1,0:T(2,128)} %early.1, s32[1,32768]{1,0:T(1,128)} %bitcast.16, s32[4,128]{1,0:T(4,128)} %bitcast.19), custom_call_target="tpu_custom_call" | custom-call | tf_op jit(solution)/shard_map/local_report/pallas_call | solution.py:272
  39.5 32.2 %exchange.1 = (f32[256,512]{1,0:T(8,128)}, f32[16,128]{1,0:T(8,128)}, f32[2,32768]{1,0:T(2,128)}) custom-call(f32[256,512]{1,0:T(8,128)} %get-tuple-element.12.hist, f32[16,128]{1,0:T(8,128)} %get-tuple-element.13.stats, f32[2,32768]{1,0:T(2,128)} %get-tuple-element.14.worst), custom_call_target="tpu_custom_call" | custom-call | tf_op jit(solution)/shard_map/exchange/pallas_call | solution.py:287
  71.8 0.0 copy-start.1
  71.8 0.0 copy-start
  71.8 2.3 %copy.24 = f32[2,2,64,512]{3,0,1,2:T(2,128)} copy(f32[2,2,64,512]{3,2,1,0:T(8,128)} %bitcast.15) | data formatting | bytes 1048576 | tf_op jit(solution)/shard_map/reshape | solution.py:302
  74.1 0.0 copy-done.1
  74.1 0.1 slice_reduce_fusion
  74.2 0.5 multiply_bitcast_fusion
  74.7 0.1 slice_reduce_fusion.1
  74.8 0.6 copy.25
  75.4 0.1 mul.38
  75.5 0.7 copy.20
  76.1 0.1 reshape_squeeze.3
  76.2 0.7 copy.21
  76.9 0.0 copy-done
  76.9 0.7 copy.27
  (2 shorter events, 0.0 us)
Async XLA Ops:
  71.8 2.3 %copy-start.1 = (f32[16,128]{1,0:T(8,128)S(1)}, f32[16,128]{1,0:T(8,128)}, u32[]{:S(2)}) copy-start(f32[16,128]{1,0:T(8,128)} %get-tuple-element.16) | copy-start | bytes 24580
  71.8 5.1 %copy-start = (f32[2,32768]{1,0:T(2,128)S(1)}, f32[2,32768]{1,0:T(2,128)}, u32[]{:S(2)}) copy-start(f32[2,32768]{1,0:T(2,128)} %get-tuple-element.49) | copy-start | bytes 786436

commit v2 on v1

v2 whole, which is shorter than its diff:
```python
import functools
import jax
import jax.numpy as jnp
from jax import lax
from jax.experimental import pallas as pl
from jax.experimental.pallas import tpu as pltpu
from jax.sharding import PartitionSpec as P

GROUPS = 64
HIGH = 4
LANES = 128
EXTRA = 16
HALF = 1024
DEPTH = 4096
MESH = pl.DeviceIdType.MESH


def pick(table, index):
    return jnp.take_along_axis(table, index, axis=1, mode="promise_in_bounds")


def make_tables(edges_ref):
    nodes = edges_ref[...].astype(jnp.float32) * 0.001
    lane = lax.broadcasted_iota(jnp.int32, (8, LANES), 1)
    rows = [jnp.broadcast_to(nodes[q : q + 1], (8, LANES)) for q in range(4)]
    third = []
    for j in range(8):
        index = (8 * lane + j) & 127
        parts = [pick(row, index) for row in rows]
        value = parts[3]
        for q in (2, 1, 0):
            value = jnp.where(lane < 16 * (q + 1), parts[q], value)
        third.append(value)
    following = pick(third[0], jnp.minimum(lane + 1, LANES - 1))
    third.append(jnp.where(lane >= 63, 0.0, following))
    second = [pick(third[0], (8 * lane + j) & 63) for j in range(1, 8)]
    first = [pick(third[0], jnp.full((8, LANES), 8 * i, jnp.int32)) for i in range(1, 8)]
    lowest = pick(third[0], jnp.zeros((8, LANES), jnp.int32))
    return first, second, third, lowest


def search(tables, slack):
    first, second, third, lowest = tables
    level = jnp.minimum(jnp.maximum(slack, lowest), 0.0)
    group = jnp.zeros(level.shape, jnp.int32)
    for bound in first:
        group += (level >= bound).astype(jnp.int32)
    finer = group * 8
    for table in second:
        finer += (level >= pick(table, group)).astype(jnp.int32)
    index = finer * 8
    low = pick(third[0], finer)
    high = pick(third[8], finer)
    inner = [pick(table, finer) for table in third[1:8]]
    for value in inner:
        above = level >= value
        index += above.astype(jnp.int32)
        low = jnp.where(above, value, low)
    for value in reversed(inner):
        high = jnp.where(level < value, value, high)
    scale = 1.0 / (high - low)
    return index, (high - level) * scale, (level - low) * scale


def search_kernel(req, arr, hreq, early, ids, edges, marks_out, worst_out, least_out):
    corners, rows = req.shape
    combos = 2 * corners
    halves = 8 // combos
    depth = halves * HALF
    tables = make_tables(edges)

    def block(step, smallest):
        slabs, parts, spans = [], [], []
        for half in range(halves):
            at = pl.ds(pl.multiple_of(step * depth + half * HALF, HALF), HALF)
            setup = req[:, at] - arr[:, at]
            hold = early[:, at] - hreq[:, at]
            worst_out[0:1, at] = jnp.min(setup, axis=0, keepdims=True)
            worst_out[1:2, at] = jnp.min(hold, axis=0, keepdims=True)
            slabs += [setup, hold]
            parts.append(jnp.broadcast_to(ids[:, at], (combos, HALF)))
            spans.append(at)
        slab = jnp.concatenate(slabs, axis=0)
        part = jnp.concatenate(parts, axis=0)
        low_at, code, w_first, w_second = [], [], [], []
        for lane in range(0, HALF, LANES):
            piece = slab[:, lane : lane + LANES]
            smallest = jnp.minimum(smallest, piece)
            index, wa, wb = search(tables, piece)
            low_at.append((index & (LANES - 1)).astype(jnp.float32))
            code.append(((index >> 7) * GROUPS + part[:, lane : lane + LANES]).astype(jnp.float32))
            w_first.append(wa)
            w_second.append(wb)
        marks = [jnp.concatenate(v, axis=1) for v in (low_at, code, w_first, w_second)]
        marks.append(jnp.minimum(slab, 0.0))
        for q, v in enumerate(marks):
            for half in range(halves):
                marks_out[q, :, spans[half]] = v[half * combos : (half + 1) * combos]
        return smallest

    start = jnp.full((8, LANES), jnp.inf, jnp.float32)
    smallest = lax.fori_loop(0, rows // depth, block, start)
    least_out[...] = jnp.broadcast_to(jnp.min(smallest, axis=1, keepdims=True), (8, LANES))


def report_kernel(
    n, nc, density,
    marks, worst, least, hist_out, stats_out, worst_out,
    acc, hist, hist_in, stats, stats_in, worst_in,
    hs, hr, gs, gr, ss, sr, ws, wr, vs, vr,
):
    combos, rows = marks.shape[1:]
    me = lax.axis_index("ep")
    mc = lax.axis_index("corner")
    chunk = GROUPS // n
    width = worst.shape[1] // nc
    narrow = jnp.bfloat16
    barrier = pltpu.get_barrier_semaphore()
    for d in range(1, n):
        pl.semaphore_signal(
            barrier, inc=1, device_id={"ep": lax.rem(me + d, n)}, device_id_type=MESH
        )
    for d in range(1, nc):
        pl.semaphore_signal(
            barrier, inc=1, device_id={"corner": lax.rem(mc + d, nc)}, device_id_type=MESH
        )
    pl.semaphore_wait(barrier, n - 1 + nc - 1)

    def send(src, dst, s_sem, r_sem, target):
        copy = pltpu.make_async_remote_copy(
            src_ref=src, dst_ref=dst, send_sem=s_sem, recv_sem=r_sem,
            device_id=target, device_id_type=MESH,
        )
        copy.start()
        return copy

    def lanes(k):
        return pl.ds(pl.multiple_of(k * width, LANES), width)

    mins = []
    for d in range(1, nc):
        t = lax.rem(mc + d, nc)
        mins.append(
            send(worst.at[:, lanes(t)], worst_in.at[d], ws.at[d], wr.at[d], {"corner": t})
        )

    iota_low = lax.broadcasted_iota(jnp.int32, (16, DEPTH), 0).astype(jnp.float32).astype(narrow)
    zero = jnp.zeros((16, DEPTH), narrow)
    one = jnp.ones((16, DEPTH), narrow)

    def product(r, first, last):
        def block(step, carry):
            at = pl.ds(pl.multiple_of(step * DEPTH, DEPTH), DEPTH)

            def row(q):
                return marks[q, r : r + 1, at]

            def spread(v):
                return jnp.broadcast_to(v, (16, DEPTH)).astype(narrow)

            at_low, at_code, wa, wb = (spread(row(q)) for q in range(4))
            neg = row(4)
            piece_a = neg.astype(narrow).astype(jnp.float32)
            rest = neg - piece_a
            piece_b = rest.astype(narrow).astype(jnp.float32)
            piece_c = rest - piece_b
            left = []
            for start in range(0, LANES, 16):
                left.append(
                    jnp.where(
                        at_low == iota_low + narrow(start),
                        wa,
                        jnp.where(at_low == iota_low + narrow(start - 1), wb, zero),
                    )
                )
            tail = jnp.where(at_low == narrow(LANES - 1), wb, zero)
            tail = jnp.where(iota_low == narrow(0), tail, zero)
            for place, v in ((1, piece_a), (2, piece_b), (3, piece_c)):
                tail = jnp.where(iota_low == narrow(place), spread(v), tail)
            left.append(jnp.where(iota_low == narrow(4), one, tail))
            right = [
                jnp.where(at_code == iota_low + narrow(start), one, zero)
                for start in range(0, HIGH * GROUPS, 16)
            ]
            acc[...] += lax.dot_general(
                jnp.concatenate(left, axis=0),
                jnp.concatenate(right, axis=0),
                (((1,), (1,)), ((), ())),
                preferred_element_type=jnp.float32,
            )
            return carry

        lax.fori_loop(first, last, block, 0)

    lane = lax.broadcasted_iota(jnp.int32, (1, HIGH * GROUPS), 1)

    def fold(v):
        v = v[:, :LANES] + v[:, LANES:]
        return v + pltpu.roll(jnp.broadcast_to(v, (8, LANES)), GROUPS, 1)[0:1]

    def settle(r):
        full = acc[...]
        over = jnp.broadcast_to(full[LANES : LANES + 1], (8, HIGH * GROUPS))
        over = pltpu.roll(over, GROUPS, 1)[0:1]
        acc[0:1] = full[0:1] + jnp.where(lane >= GROUPS, over, 0.0)
        turned = acc[0:LANES].T
        for k in range(n):
            for g in range(HIGH):
                top = g * GROUPS + k * chunk
                hist[r, k, :, g * LANES : (g + 1) * LANES] = turned[top : top + chunk]
        pieces = [full[LANES + 1 + i : LANES + 2 + i] for i in range(3)]
        stats[r : r + 1] = fold(pieces[0] + pieces[1] + pieces[2])
        if r == 0:
            stats[combos : combos + 1] = fold(full[LANES + 4 : LANES + 5])

    def scatter(r):
        copies = []
        for d in range(1, n):
            t = lax.rem(me + d, n)
            copies.append(
                send(hist.at[r, t], hist_in.at[r, d], hs.at[r, d], hr.at[r, d], {"ep": t})
            )
        return copies

    def gather(r, scattered):
        total = hist[r, me]
        for d in range(1, n):
            scattered[d - 1].wait_recv()
            total += hist_in[r, d]
        hist_out[r, me] = total * density
        copies = []
        for d in range(1, n):
            t = lax.rem(me + d, n)
            part = hist_out.at[r, me]
            copies.append(send(part, part, gs.at[r, d], gr.at[r, d], {"ep": t}))
        return copies

    steps = rows // DEPTH
    stats[...] = jnp.zeros_like(stats)
    stats[8:16] = least[...]
    sent, spread_out, gathered = [], [], []
    for r in range(combos):
        acc[...] = jnp.zeros_like(acc)
        product(r, 0, steps // 2)
        if r == 0:
            for copy in mins:
                copy.wait_recv()
            low = worst[:, lanes(mc)]
            for d in range(1, nc):
                low = jnp.minimum(low, worst_in[d])
            worst_out[:, lanes(mc)] = low
            for d in range(1, nc):
                t = lax.rem(mc + d, nc)
                part = worst_out.at[:, lanes(mc)]
                spread_out.append(send(part, part, vs.at[d], vr.at[d], {"corner": t}))
        else:
            gathered += gather(r - 1, sent[-1])
        product(r, steps // 2, steps)
        settle(r)
        sent.append(scatter(r))
    shares = []
    for d in range(1, n):
        t = lax.rem(me + d, n)
        shares.append(send(stats, stats_in.at[me], ss.at[d], sr.at[d], {"ep": t}))
    gathered += gather(combos - 1, sent[-1])
    for copy in shares:
        copy.wait_recv()
    stats_in[me] = stats[...]
    added = stats_in[0, 0:8]
    lowest = stats_in[0, 8:16]
    for k in range(1, n):
        added += stats_in[k, 0:8]
        lowest = jnp.minimum(lowest, stats_in[k, 8:16])
    stats_out[0:8] = added
    stats_out[8:16] = lowest
    for copy in spread_out + gathered:
        copy.wait_recv()
    for copy in mins + sum(sent, []) + shares + spread_out + gathered:
        copy.wait_send()


def on_device(required, arrival, hold_required, early_arrival, part_ids, bin_edges):
    corners, rows = required.shape
    n, nc = lax.axis_size("ep"), lax.axis_size("corner")
    endpoints = rows * n
    bins = bin_edges.shape[0]
    combos = 2 * corners
    f32 = jnp.float32
    vmem = pl.BlockSpec(memory_space=pltpu.VMEM)
    marks, worst, least = pl.pallas_call(
        search_kernel,
        out_shape=(
            jax.ShapeDtypeStruct((5, combos, rows), f32),
            jax.ShapeDtypeStruct((2, rows), f32),
            jax.ShapeDtypeStruct((8, LANES), f32),
        ),
        in_specs=[vmem] * 6,
        out_specs=[vmem] * 3,
        name="node_search",
    )(
        required, arrival, hold_required, early_arrival,
        part_ids.reshape(1, rows), bin_edges.reshape(bins // LANES, LANES),
    )
    dma = pltpu.SemaphoreType.DMA
    blocks = (combos, n, GROUPS // n, bins)
    hist, stats, worst = pl.pallas_call(
        functools.partial(report_kernel, n, nc, GROUPS * bins / endpoints),
        out_shape=(
            jax.ShapeDtypeStruct(blocks, f32),
            jax.ShapeDtypeStruct((16, LANES), f32),
            jax.ShapeDtypeStruct((2, rows), f32),
        ),
        in_specs=[vmem] * 3,
        out_specs=[vmem] * 3,
        scratch_shapes=[
            pltpu.VMEM((LANES + EXTRA, HIGH * GROUPS), f32),
            pltpu.VMEM(blocks, f32),
            pltpu.VMEM(blocks, f32),
            pltpu.VMEM((16, LANES), f32),
            pltpu.VMEM((n, 16, LANES), f32),
            pltpu.VMEM((nc, 2, rows // nc), f32),
        ]
        + [dma((combos, n))] * 4
        + [dma((n,))] * 2
        + [dma((nc,))] * 4,
        compiler_params=pltpu.CompilerParams(collective_id=0, has_side_effects=True),
        name="report",
    )(marks, worst, least)
    part_hist = hist.reshape(2, corners, GROUPS, bins).transpose(2, 1, 0, 3)
    share = GROUPS / endpoints
    sums = stats[:combos, :GROUPS].reshape(2, corners, GROUPS)
    part_tns = sums.transpose(2, 1, 0) * share
    part_share = stats[combos, :GROUPS] * share
    tns = jnp.sum(sums, axis=2).T * (1.0 / endpoints)
    least = jnp.min(stats[8:16, 0].reshape(8 // combos, 2, corners), axis=0)
    return (part_hist, part_tns, part_share, tns, least.T, worst)


def solution(mesh):
    in_specs = (
        P("corner", "ep"),
        P("corner", "ep"),
        P("corner", "ep"),
        P("corner", "ep"),
        P("ep"),
        P(),
    )
    out_specs = (
        P(None, "corner", None, None),
        P(None, "corner", None),
        P(),
        P("corner", None),
        P("corner", None),
        P(None, "ep"),
    )
    return jax.shard_map(
        on_device, mesh=mesh, in_specs=in_specs, out_specs=out_specs, check_vma=False
    )
```

time: 77.8 us -> 71.9 us (0.924)
  the two profiles are of different devices: /device:TPU:31 before, /device:TPU:0 now
where the time goes in v2:
time: 71.9 us; the launch traced here: 71.6 us
  Pallas kernels  62.2 us (87%)
  local copies, waits for them, and re-layouts  6.75 us (9%)
  other arithmetic  2.01 us (3%)
    pallas_call x1, Pallas kernels, on_device(): pl.pallas_call(functools.partial(report_kernel, n, nc, GROUPS * bins / en...  52 us
    pallas_call x1, Pallas kernels, on_device(): pl.pallas_call(search_kernel, out_shape=(jax.ShapeDtypeStruct((5, combos,...  10.1 us
    unnamed x3, local copies, waits for them, and re-layouts  2.97 us
    reshape x1, local copies, waits for them, and re-layouts, on_device(): part_hist = hist.reshape(2, corners, GROUPS, bins).transpose(2, 1, 0, 3)  2.24 us

profile of v2, /device:TPU:0, one launch (start us, length us, event | category | flops | bytes accessed | tf_op | source)
XLA Modules:
  0.0 71.6 jit_solution(994745260623351048)
XLA Ops:
  0.6 10.1 %node_search.1 = (f32[5,4,32768]{2,1,0:T(4,128)}, f32[2,32768]{1,0:T(2,128)}, f32[8,128]{1,0:T(8,128)}) custom-call(f32[2,32768]{1,0:T(2,128)} %req.1, f32[2,32768]{1,0:T(2,128)} %arr.1, f32[2,32768]{1,0:T(2,128)} %hreq.1, f32[2,32768]{1,0:T(2,128)} %early.1, s32[1,32768]{1,0:T(1,128)} %bitcast.16, s32[4,128]{1,0:T(4,128)} %bitcast.19), custom_call_target="tpu_custom_call" | custom-call | tf_op jit(solution)/shard_map/node_search/pallas_call | solution.py:290
  10.8 52.0 %report.1 = (f32[4,8,8,512]{3,2,1,0:T(8,128)}, f32[16,128]{1,0:T(8,128)}, f32[2,32768]{1,0:T(2,128)}) custom-call(f32[5,4,32768]{2,1,0:T(4,128)} %get-tuple-element.12.marks, f32[2,32768]{1,0:T(2,128)} %get-tuple-element.13.worst, f32[8,128]{1,0:T(8,128)} %get-tuple-element.14.least), custom_call_target="tpu_custom_call" | custom-call | tf_op jit(solution)/shard_map/report/pallas_call | solution.py:306
  62.8 2.2 %copy.24 = f32[2,2,64,512]{3,0,1,2:T(2,128)} copy(f32[2,2,64,512]{3,2,1,0:T(8,128)} %bitcast.15) | data formatting | bytes 1048576 | tf_op jit(solution)/shard_map/reshape | solution.py:329
  65.0 0.8 %slice_reduce_fusion = f32[8]{0:T(128)S(1)} fusion(f32[16,128]{1,0:T(8,128)} %get-tuple-element.16), kind=kLoop, calls=%fused_computation.1 | loop fusion | bytes 64 | tf_op jit(solution)/shard_map/slice | solution.py:335
  65.8 1.2 %multiply_bitcast_fusion = f32[64]{0:T(128)} fusion(f32[16,128]{1,0:T(8,128)} %get-tuple-element.16), kind=kLoop, calls=%fused_computation.5 | loop fusion | flops 64 | bytes 512 | tf_op jit(solution)/shard_map/mul | solution.py:333
  67.0 0.8 %slice_reduce_fusion.1 = (f32[4]{0:T(128)S(1)}, f32[4,64]{1,0:T(4,128)S(1)}) fusion(f32[16,128]{1,0:T(8,128)} %get-tuple-element.16), kind=kLoop, calls=%fused_computation.3 | loop fusion | flops 508 | bytes 2064 | tf_op jit(solution)/shard_map/reduce_sum | solution.py:334
  67.8 0.6 copy.25
  68.4 0.1 mul.38
  68.5 0.7 copy.20
  69.1 0.1 reshape_squeeze.3
  69.2 0.7 copy.21
  69.9 1.7 %copy.27 = f32[2,32768]{1,0:T(2,128)} copy(f32[2,32768]{1,0:T(2,128)} %get-tuple-element.49) | data formatting | bytes 524288
  (2 shorter events, 0.0 us)

commit v3 on v2

--- a/solution.py
+++ b/solution.py
@@ -277,6 +277,26 @@
         copy.wait_recv()
     for copy in mins + sum(sent, []) + shares + spread_out + gathered:
         copy.wait_send()
+
+
+def finish_kernel(endpoints, hist, stats, worst, hist_out, tns_out, share_out, total_out, least_out, worst_out):
+    corners = total_out.shape[0]
+    combos = 2 * corners
+    share = GROUPS / endpoints
+    for m in range(2):
+        for c in range(corners):
+            r = m * corners + c
+            hist_out[:, c, m, :] = hist[r]
+            row = stats[r : r + 1, :GROUPS]
+            tns_out[c, m : m + 1, :] = row * share
+            total = jnp.sum(row, axis=1, keepdims=True) * (1.0 / endpoints)
+            total_out[c : c + 1, m : m + 1] = total
+            low = stats[8 + r : 9 + r, 0:1]
+            for top in range(8 + combos, 16, combos):
+                low = jnp.minimum(low, stats[top + r : top + r + 1, 0:1])
+            least_out[c : c + 1, m : m + 1] = low
+    share_out[...] = stats[combos : combos + 1, :GROUPS] * share
+    worst_out[...] = worst[...]
 
 
 def on_device(required, arrival, hold_required, early_arrival, part_ids, bin_edges):
@@ -326,14 +346,21 @@
         compiler_params=pltpu.CompilerParams(collective_id=0, has_side_effects=True),
         name="report",
     )(marks, worst, least)
-    part_hist = hist.reshape(2, corners, GROUPS, bins).transpose(2, 1, 0, 3)
-    share = GROUPS / endpoints
-    sums = stats[:combos, :GROUPS].reshape(2, corners, GROUPS)
-    part_tns = sums.transpose(2, 1, 0) * share
-    part_share = stats[combos, :GROUPS] * share
-    tns = jnp.sum(sums, axis=2).T * (1.0 / endpoints)
-    least = jnp.min(stats[8:16, 0].reshape(8 // combos, 2, corners), axis=0)
-    return (part_hist, part_tns, part_share, tns, least.T, worst)
+    part_hist, part_tns, part_share, tns, wns, worst = pl.pallas_call(
+        functools.partial(finish_kernel, endpoints),
+        out_shape=(
+            jax.ShapeDtypeStruct((GROUPS, corners, 2, bins), f32),
+            jax.ShapeDtypeStruct((corners, 2, GROUPS), f32),
+            jax.ShapeDtypeStruct((1, GROUPS), f32),
+            jax.ShapeDtypeStruct((corners, 2), f32),
+            jax.ShapeDtypeStruct((corners, 2), f32),
+            jax.ShapeDtypeStruct((2, rows), f32),
+        ),
+        in_specs=[vmem] * 3,
+        out_specs=[vmem] * 6,
+        name="finish",
+    )(hist.reshape(combos, GROUPS, bins), stats, worst)
+    return (part_hist, part_tns.transpose(2, 0, 1), part_share[0], tns, wns, worst)
 
 
 def solution(mesh):

time: 71.9 us -> 65.1 us (0.905)
  local copies, waits for them, and re-layouts: 6.75 us -> 0 us
  other arithmetic: 2.01 us -> 0 us
  Pallas kernels: 62.2 us -> 64.2 us
    unnamed x3 -> x0, local copies, waits for them, and re-layouts: 2.97 us -> none
    reshape x1 -> x0, local copies, waits for them, and re-layouts: 2.24 us -> none  [on_device(): part_hist = hist.reshape(2, corners, GROUPS, bins).transpose(2, 1, 0, 3)]
    pallas_call x0 -> x1, Pallas kernels: none -> 2.11 us  [on_device(): pl.pallas_call(functools.partial(finish_kernel, endpoints), out_shape=(ja...]
    mul x2 -> x0, other arithmetic: 1.2 us -> none  [the longest x1 1.19 us: on_device(): part_share = stats[combos, :GROUPS] * share]
    slice x1 -> x0, local copies, waits for them, and re-layouts: 0.8 us -> none  [on_device(): least = jnp.min(stats[8:16, 0].reshape(8 // combos, 2, corners), axis=0)]
    reduce_sum x1 -> x0, other arithmetic: 0.79 us -> none  [on_device(): tns = jnp.sum(sums, axis=2).T * (1.0 / endpoints)]
where the time goes in v3:
time: 65.1 us; the launch traced here: 64.9 us
  Pallas kernels  64.2 us (99%)
    pallas_call x1, Pallas kernels, on_device(): pl.pallas_call(functools.partial(report_kernel, n, nc, GROUPS * bins / en...  52 us
    pallas_call x1, Pallas kernels, on_device(): pl.pallas_call(search_kernel, out_shape=(jax.ShapeDtypeStruct((5, combos,...  10.1 us
    pallas_call x1, Pallas kernels, on_device(): pl.pallas_call(functools.partial(finish_kernel, endpoints), out_shape=(ja...  2.11 us

profile of v3, /device:TPU:0, one launch (start us, length us, event | category | flops | bytes accessed | tf_op | source)
XLA Modules:
  0.0 64.9 jit_solution(13851009084064597722)
XLA Ops:
  0.6 10.1 %node_search.1 = (f32[5,4,32768]{2,1,0:T(4,128)}, f32[2,32768]{1,0:T(2,128)}, f32[8,128]{1,0:T(8,128)}) custom-call(f32[2,32768]{1,0:T(2,128)} %req.1, f32[2,32768]{1,0:T(2,128)} %arr.1, f32[2,32768]{1,0:T(2,128)} %hreq.1, f32[2,32768]{1,0:T(2,128)} %early.1, s32[1,32768]{1,0:T(1,128)} %bitcast.6, s32[4,128]{1,0:T(4,128)} %bitcast.7), custom_call_target="tpu_custom_call" | custom-call | tf_op jit(solution)/shard_map/node_search/pallas_call | solution.py:310
  10.8 52.0 %report.1 = (f32[4,8,8,512]{3,2,1,0:T(8,128)}, f32[16,128]{1,0:T(8,128)}, f32[2,32768]{1,0:T(2,128)}) custom-call(f32[5,4,32768]{2,1,0:T(4,128)} %get-tuple-element.18.marks, f32[2,32768]{1,0:T(2,128)} %get-tuple-element.19.worst, f32[8,128]{1,0:T(8,128)} %get-tuple-element.20.least), custom_call_target="tpu_custom_call" | custom-call | tf_op jit(solution)/shard_map/report/pallas_call | solution.py:326
  62.8 2.1 %finish.1 = (f32[64,2,2,512]{3,2,1,0:T(2,128)}, f32[2,2,64]{2,1,0:T(2,128)}, f32[1,64]{1,0:T(1,128)}, f32[2,2]{1,0:T(2,128)}, f32[2,2]{1,0:T(2,128)}, /*index=5*/f32[2,32768]{1,0:T(2,128)}) custom-call(f32[4,64,512]{2,1,0:T(8,128)} %bitcast.5, f32[16,128]{1,0:T(8,128)} %get-tuple-element.22.stats, f32[2,32768]{1,0:T(2,128)} %get-tuple-element.23.worst), custom_call_target="tpu_custom_call" | custom-call | tf_op jit(solution)/shard_map/finish/pallas_call | solution.py:349
